TPU v7x, 256 devices: a whole 4x4x8 slice. The times are simulated.
256 devices in a mesh: dp: 2 (over x_lo), fsdp: 16 (over x_hi, y, core), tensor: 8 (over z).
Axes of the slice: x: 4 (x_hi: 2, x_lo: 2; x = x_hi * 2 + x_lo), y: 4, z: 8, core: 2. Of those that a mesh axis runs over, the one named last changes fastest.
Arguments:
- hidden: bfloat16 [16384, 2048], P(('dp', 'fsdp'), 'tensor'), may hold values from -8 to 8
- norm_gain: bfloat16 [2048], P('tensor'), may hold values from 0.099609375 to 1.8984375
- head_weight: bfloat16 [2048, 32128], P('fsdp', 'tensor'), may hold values from -1 to 1
- token_ids: int32 [32, 512], P(('dp', 'fsdp')), may hold values from 0 to 32127
- lengths: int32 [32], P(('dp', 'fsdp')), may hold values from 128 to 512
- old_logp: float32 [32, 512], P(('dp', 'fsdp')), may hold values from -12.5 to -9.5
- advantages: float32 [32, 512], P(('dp', 'fsdp')), may hold values from -4 to 4
- rollout_logp: float32 [32, 512], P(('dp', 'fsdp'), 'tensor'), may hold values from -16 to -1
- rollout_row: int32 [32], P(('dp', 'fsdp')), may hold values from 0 to 31, each once
Outputs:
- new_logp: float32 [32, 512], P(('dp', 'fsdp'))
- token_loss: float32 [32, 512], P(('dp', 'fsdp'))
- summary: float32 [3], replicated
Inputs may be any that keep to these rules, and one draw needn't show every extreme that they name: `rollout_row`: every row 0 to 31 is named once.
All inputs are finite; a program needn't handle non-finite values.
Results may differ from a plain program's by a relative error of at most 0.0005.
The roundings to bfloat16 on the way count: a program that leaves them out, or rounds other values in their place, can miss the bound.
Values may be sent and summed in bfloat16 or wider, within the bound.
A program may use at most 128 MiB of HBM per device.

v0:
```python
import jax
import jax.numpy as jnp
from jax import lax
from jax.sharding import PartitionSpec as P

clip_eps = 0.2
kl_coef = 0.2
log_limit = 10.0
norm_eps = 1e-06


def copy_for_each(array, axis):
    copies = jnp.broadcast_to(array, (lax.axis_size(axis), *array.shape))
    return lax.all_to_all(copies, axis, split_axis=0, concat_axis=0, tiled=True)


def taken_together(array, axis):
    everything = copy_for_each(array, axis)
    return jnp.max(everything, axis=0)


def taken_together_2(array, axis):
    everything = copy_for_each(array, axis)
    return jnp.sum(everything, axis=0)


def in_one(arrays, axis):
    line, at, outs = (jnp.concatenate([a.reshape(-1) for a in arrays]), 0, [])
    so_far = taken_together_2(line, axis)
    for a in arrays:
        outs.append(so_far[at : at + a.size].reshape(a.shape))
        at += a.size
    return tuple(outs)


def joined_along(tiles, dim):
    lengths = list(tiles.shape[1:])
    lengths[dim] *= tiles.shape[0]
    return jnp.moveaxis(tiles, 0, dim).reshape(lengths)


def collect(array, axis, dim):
    return joined_along(copy_for_each(array, axis), dim)


def token_terms(new_logp, old_logp, advantages, ref_logp, live_mask, prob_square):
    shift = new_logp - old_logp
    prob_ratio = jnp.exp(jnp.clip(shift, -log_limit, log_limit))
    clipped = jnp.clip(prob_ratio, 1.0 - clip_eps, 1.0 + clip_eps)
    plain_term = prob_ratio * advantages
    bounded_term = clipped * advantages
    surrogate = jnp.minimum(plain_term, bounded_term)
    ref_gap = ref_logp - new_logp
    gap_clip = jnp.clip(ref_gap, -log_limit, log_limit)
    kl_term = jnp.exp(gap_clip) - gap_clip - 1.0
    token_loss = live_mask * (kl_coef * kl_term - surrogate)
    inside_gap = (jnp.abs(ref_gap) < log_limit).astype(jnp.float32)
    inside_ratio = (jnp.abs(shift) < log_limit).astype(jnp.float32)
    active_term = (plain_term <= bounded_term).astype(jnp.float32)
    grad_coef = live_mask * (
        kl_coef * (1.0 - jnp.exp(gap_clip)) * inside_gap
        - advantages * prob_ratio * active_term * inside_ratio
    )
    grad_square = grad_coef * grad_coef * (prob_square - 2.0 * jnp.exp(new_logp) + 1.0)
    return (token_loss, live_mask * kl_term, grad_square)


def exp_sums(logits, row_max):
    shifted = jnp.exp(logits - row_max[:, None])
    return (jnp.sum(shifted, axis=1), jnp.sum(shifted * shifted, axis=1))


def vocab_stats(logits, flat_ids, col_start):
    col_ids = lax.broadcasted_iota(jnp.int32, logits.shape, 1) + col_start
    picked = jnp.sum(jnp.where(col_ids == flat_ids[:, None], logits, 0.0), axis=1)
    local_max = jnp.max(logits, axis=1)
    row_max = taken_together(local_max, "tensor")
    exp_sum, exp_square = exp_sums(logits, row_max)
    exp_sum, exp_square, picked = in_one((exp_sum, exp_square, picked), "tensor")
    return (row_max, exp_sum, exp_square, picked)


def shards(
    hidden,
    norm_gain,
    head_weight,
    token_ids,
    lengths,
    old_logp,
    advantages,
    rollout_logp,
    rollout_row,
):
    full_rows, full_gain = (collect(hidden, "tensor", 1), collect(norm_gain, "tensor", 0))
    values = full_rows.astype(jnp.float32)
    inv_rms = lax.rsqrt(jnp.mean(values * values, axis=1, keepdims=True) + norm_eps)
    normed = (values * inv_rms * full_gain.astype(jnp.float32)[None, :]).astype(jnp.bfloat16)
    flat_ids = token_ids.reshape(-1)
    vocab_cols = head_weight.shape[1]
    tensor_pos = lax.axis_index("tensor")
    logits = jnp.dot(
        normed,
        lax.all_gather(head_weight, "fsdp", axis=0, tiled=True),
        preferred_element_type=jnp.float32,
    )
    soft_stats = vocab_stats(logits, flat_ids, tensor_pos * vocab_cols)
    row_max, exp_sum, exp_square, picked = soft_stats
    new_logp = (picked - row_max - jnp.log(exp_sum)).reshape(token_ids.shape)
    prob_square = (exp_square / (exp_sum * exp_sum)).reshape(token_ids.shape)
    ref_all = collect(rollout_logp, ("dp", "fsdp"), 0)
    own_ref = jnp.take(ref_all, rollout_row, axis=0)
    ref_logp = collect(own_ref, "tensor", 1)
    positions = lax.broadcasted_iota(jnp.int32, token_ids.shape, 1)
    live_mask = (positions < lengths[:, None]).astype(jnp.float32)
    token_loss, kl_part, grad_part = token_terms(
        new_logp, old_logp, advantages, ref_logp, live_mask, prob_square
    )
    live_count, loss_sum, kl_sum, grad_sum = in_one(
        (jnp.sum(live_mask), jnp.sum(token_loss), jnp.sum(kl_part), jnp.sum(grad_part)),
        ("dp", "fsdp"),
    )
    summary = jnp.stack(
        [loss_sum / live_count, kl_sum / live_count, jnp.sqrt(grad_sum / live_count)]
    )
    return (new_logp, token_loss, summary)


def solution(mesh):
    in_specs = (
        P(("dp", "fsdp"), "tensor"),
        P("tensor"),
        P("fsdp", "tensor"),
        P(("dp", "fsdp"), None),
        P(("dp", "fsdp")),
        P(("dp", "fsdp"), None),
        P(("dp", "fsdp"), None),
        P(("dp", "fsdp"), "tensor"),
        P(("dp", "fsdp")),
    )
    out_specs = (P(("dp", "fsdp"), None), P(("dp", "fsdp"), None), P())
    return jax.shard_map(shards, mesh=mesh, in_specs=in_specs, out_specs=out_specs, check_vma=False)
```

profile of v0, /device:TPU:1, one launch (start us, length us, event | category | flops | bytes accessed | tf_op | source)
XLA Modules:
  0.0 218.8 jit_solution(17460148132570036709)
XLA Ops:
  7.2 0.7 all-gather.2.cloned.1.call-update
  7.9 0.7 broadcast_in_dim.42
  9.1 0.7 reduce.12
  9.8 0.6 reshape.211
  10.4 9.0 %all-to-all-start.1 = ((bf16[8,2,128]{2,1,0:T(2,128)(2,1)}), bf16[8,2,128]{2,1,0:T(2,128)(2,1)S(1)}, u32[]{:S(2)}, u32[]{:S(2)}) async-start(bf16[8,2,128]{2,1,0:T(2,128)(2,1)} %reshape.211), calls=%async_computation.1 | async-start | bytes 8192 | tf_op jit(solution)/shard_map/all_to_all | solution.py:14
  19.4 1.1 copy.14
  20.5 5.5 %all-to-all-done.1 = bf16[8,2,128]{2,1,0:T(2,128)(2,1)S(1)} async-done(((bf16[8,2,128]{2,1,0:T(2,128)(2,1)}), bf16[8,2,128]{2,1,0:T(2,128)(2,1)S(1)}, u32[]{:S(2)}, u32[]{:S(2)}) %all-to-all-start.1) | async-done | bytes 4128 | tf_op jit(solution)/shard_map/all_to_all | solution.py:14
  25.9 1.5 broadcast_in_dim.41
  27.4 3.6 %all-to-all-start = ((bf16[8,512,256]{1,2,0:T(8,128)(2,1)}), bf16[8,512,256]{1,2,0:T(8,128)(2,1)S(1)}, u32[]{:S(2)}, u32[]{:S(2)}) async-start(bf16[8,512,256]{1,2,0:T(8,128)(2,1)} %broadcast_in_dim.41), calls=%async_computation | async-start | bytes 4194304 | tf_op jit(solution)/shard_map/all_to_all | solution.py:14
  31.8 50.9 %all-to-all-done = bf16[8,512,256]{1,2,0:T(8,128)(2,1)S(1)} async-done(((bf16[8,512,256]{1,2,0:T(8,128)(2,1)}), bf16[8,512,256]{1,2,0:T(8,128)(2,1)S(1)}, u32[]{:S(2)}, u32[]{:S(2)}) %all-to-all-start) | async-done | bytes 2097184 | tf_op jit(solution)/shard_map/all_to_all | solution.py:14
  82.6 0.6 broadcast_in_dim.48
  83.2 7.6 %all-to-all-start.4 = ((f32[32,1,64]{2,1,0:T(1,128)}), f32[32,1,64]{2,1,0:T(1,128)S(1)}, u32[]{:S(2)}, u32[]{:S(2)}) async-start(f32[32,1,64]{2,1,0:T(1,128)} %broadcast_in_dim.48), calls=%async_computation.4 | async-start | bytes 32768 | tf_op jit(solution)/shard_map/all_to_all | solution.py:14
  91.4 2.0 fusion.2
  93.4 43.2 %all-gather.2.cloned.1.call-done = bf16[2048,4016]{0,1:T(8,128)(2,1)} async-done(((bf16[128,4016]{0,1:T(8,128)(2,1)}), bf16[2048,4016]{0,1:T(8,128)(2,1)}) %all-gather.2.cloned.1.call-update) | async-done | bytes 16449552 | tf_op jit(solution)/shard_map/all_gather | solution.py:103
  136.5 14.8 %fusion.18 = (f32[512]{0:T(512)S(1)}, f32[512,4016]{0,1:T(8,128)}) fusion(bf16[2048,4016]{0,1:T(8,128)(2,1)} %all-gather.2.cloned.1.call-done, bf16[512,2048]{0,1:T(8,128)(2,1)} %fusion.2), kind=kOutput, calls=%fused_computation.43 | convolution fusion | flops 8424218112 | bytes 26773504 | tf_op jit(solution)/shard_map/dot_general | solution.py:101
  151.3 0.6 broadcast_in_dim.43
  151.9 6.7 %all-to-all-start.2 = ((f32[8,1,512]{2,1,0:T(1,128)}), f32[8,1,512]{2,1,0:T(1,128)S(1)}, u32[]{:S(2)}, u32[]{:S(2)}) async-start(f32[8,1,512]{2,1,0:T(1,128)} %broadcast_in_dim.43), calls=%async_computation.2 | async-start | bytes 32768 | tf_op jit(solution)/shard_map/all_to_all | solution.py:14
  158.7 6.6 %all-to-all-done.2 = f32[8,1,512]{2,1,0:T(1,128)S(1)} async-done(((f32[8,1,512]{2,1,0:T(1,128)}), f32[8,1,512]{2,1,0:T(1,128)S(1)}, u32[]{:S(2)}, u32[]{:S(2)}) %all-to-all-start.2) | async-done | bytes 16416 | tf_op jit(solution)/shard_map/all_to_all | solution.py:14
  165.3 0.6 broadcast_in_dim.50
  165.9 3.3 %all-to-all-start.5 = ((f32[8,1,64]{2,1,0:T(1,128)}), f32[8,1,64]{2,1,0:T(1,128)S(1)}, u32[]{:S(2)}, u32[]{:S(2)}) async-start(f32[8,1,64]{2,1,0:T(1,128)} %broadcast_in_dim.50), calls=%async_computation.5 | async-start | bytes 8192 | tf_op jit(solution)/shard_map/all_to_all | solution.py:14
  169.3 5.4 %fusion = (f32[512]{0:T(512)S(1)}, f32[512]{0:T(512)S(1)}, f32[512]{0:T(512)S(1)}) fusion(f32[512,4016]{0,1:T(8,128)} %get-tuple-element.29, f32[512]{0:T(512)S(1)} %reduce_max.19, s32[512]{0:T(512)S(1)} %bitcast.36, s32[4016]{0:T(1024)S(1)} %iota_add_fusion), kind=kLoop, calls=%fused_computation.3 | loop fusion | flops 14391808 | bytes 8251072 | tf_op jit(solution)/shard_map/reduce_sum | solution.py:70
  174.7 1.0 all-to-all-done.5
  175.7 0.6 broadcast_in_dim.45
  176.3 5.6 %all-to-all-start.3 = ((f32[8,1,1536]{2,1,0:T(1,128)}), f32[8,1,1536]{2,1,0:T(1,128)S(1)}, u32[]{:S(2)}, u32[]{:S(2)}) async-start(f32[8,1,1536]{2,1,0:T(1,128)} %broadcast_in_dim.45), calls=%async_computation.3 | async-start | bytes 98304 | tf_op jit(solution)/shard_map/all_to_all | solution.py:14
  183.1 0.7 reduce.11
  183.9 5.1 %all-to-all-done.3 = f32[8,1,1536]{2,1,0:T(1,128)S(1)} async-done(((f32[8,1,1536]{2,1,0:T(1,128)}), f32[8,1,1536]{2,1,0:T(1,128)S(1)}, u32[]{:S(2)}, u32[]{:S(2)}) %all-to-all-start.3) | async-done | bytes 49184 | tf_op jit(solution)/shard_map/all_to_all | solution.py:14
  189.2 0.6 reduce_sum.97
  189.8 1.3 fusion.15
  191.1 2.6 %pad_maximum_fusion.1 = f32[4]{0:T(128)S(1)} fusion(f32[1]{0:T(128)} %bitcast.17, f32[1]{0:T(128)} %bitcast.14, f32[1]{0:T(128)} %bitcast.12, f32[1]{0:T(128)} %bitcast.11), kind=kLoop, calls=%fused_computation.38 | loop fusion | flops 12 | bytes 32 | tf_op jit(solution)/shard_map/concatenate | solution.py:28
  193.7 13.1 %all_to_all.39 = f32[32,1,4]{2,1,0:T(1,128)S(1)} all-to-all(f32[32,1,4]{2,1,0:T(1,128)S(1)} %broadcast_in_dim.51), channel_id=1, replica_groups=mesh['dp'=2,'fsdp'=16,'tensor'=8] {'dp','fsdp'}, dimensions={0} | all-to-all | bytes 1024 | tf_op jit(solution)/shard_map/all_to_all | solution.py:14
  206.9 0.7 fusion.17
  211.3 0.6 pad_maximum_fusion.2
  (30 shorter events, 2.0 us)
Async XLA Ops:
  7.2 75.5 %copy-start.4 = (f32[1,64]{1,0:T(1,128)S(1)}, f32[1,64]{1,0:T(1,128)}, u32[]{:S(2)}) copy-start(f32[1,64]{1,0:T(1,128)} %param.16) | copy-start | bytes 772
  7.2 129.3 %all-gather.2.cloned.1.call-start = ((), (), s32[]{:S(2)}) async-start(), calls=%async_computation.7 | async-start | bytes 17477632 | tf_op jit(solution)/shard_map/all_gather | solution.py:103
  10.4 15.6 %all-to-all-start.1 = ((bf16[8,2,128]{2,1,0:T(2,128)(2,1)}), bf16[8,2,128]{2,1,0:T(2,128)(2,1)S(1)}, u32[]{:S(2)}, u32[]{:S(2)}) async-start(bf16[8,2,128]{2,1,0:T(2,128)(2,1)} %reshape.211), calls=%async_computation.1 | async-start | bytes 8192 | tf_op jit(solution)/shard_map/all_to_all | solution.py:14
  27.4 55.2 %all-to-all-start = ((bf16[8,512,256]{1,2,0:T(8,128)(2,1)}), bf16[8,512,256]{1,2,0:T(8,128)(2,1)S(1)}, u32[]{:S(2)}, u32[]{:S(2)}) async-start(bf16[8,512,256]{1,2,0:T(8,128)(2,1)} %broadcast_in_dim.41), calls=%async_computation | async-start | bytes 4194304 | tf_op jit(solution)/shard_map/all_to_all | solution.py:14
  83.2 68.1 %all-to-all-start.4 = ((f32[32,1,64]{2,1,0:T(1,128)}), f32[32,1,64]{2,1,0:T(1,128)S(1)}, u32[]{:S(2)}, u32[]{:S(2)}) async-start(f32[32,1,64]{2,1,0:T(1,128)} %broadcast_in_dim.48), calls=%async_computation.4 | async-start | bytes 32768 | tf_op jit(solution)/shard_map/all_to_all | solution.py:14
  93.4 75.9 %copy-start.3 = (s32[1,512]{1,0:T(1,128)S(1)}, s32[1,512]{1,0:T(1,128)}, u32[]{:S(2)}) copy-start(s32[1,512]{1,0:T(1,128)} %param.12) | copy-start | bytes 6148
  151.9 13.4 %all-to-all-start.2 = ((f32[8,1,512]{2,1,0:T(1,128)}), f32[8,1,512]{2,1,0:T(1,128)S(1)}, u32[]{:S(2)}, u32[]{:S(2)}) async-start(f32[8,1,512]{2,1,0:T(1,128)} %broadcast_in_dim.43), calls=%async_computation.2 | async-start | bytes 32768 | tf_op jit(solution)/shard_map/all_to_all | solution.py:14
  165.9 9.8 %all-to-all-start.5 = ((f32[8,1,64]{2,1,0:T(1,128)}), f32[8,1,64]{2,1,0:T(1,128)S(1)}, u32[]{:S(2)}, u32[]{:S(2)}) async-start(f32[8,1,64]{2,1,0:T(1,128)} %broadcast_in_dim.50), calls=%async_computation.5 | async-start | bytes 8192 | tf_op jit(solution)/shard_map/all_to_all | solution.py:14
  169.3 20.6 %copy-start.1 = (f32[1,512]{1,0:T(1,128)S(1)}, f32[1,512]{1,0:T(1,128)}, u32[]{:S(2)}) copy-start(f32[1,512]{1,0:T(1,128)} %param.15) | copy-start | bytes 6148
  169.3 20.6 %copy-start.2 = (f32[1,512]{1,0:T(1,128)S(1)}, f32[1,512]{1,0:T(1,128)}, u32[]{:S(2)}) copy-start(f32[1,512]{1,0:T(1,128)} %param.14) | copy-start | bytes 6148
  176.3 12.7 %all-to-all-start.3 = ((f32[8,1,1536]{2,1,0:T(1,128)}), f32[8,1,1536]{2,1,0:T(1,128)S(1)}, u32[]{:S(2)}, u32[]{:S(2)}) async-start(f32[8,1,1536]{2,1,0:T(1,128)} %broadcast_in_dim.45), calls=%async_computation.3 | async-start | bytes 98304 | tf_op jit(solution)/shard_map/all_to_all | solution.py:14
  189.1 22.9 %copy-start = (f32[512]{0:T(512)}, f32[512]{0:T(512)S(1)}, u32[]{:S(2)}) copy-start(f32[512]{0:T(512)S(1)} %get-tuple-element.20) | copy-start | bytes 6148
Sparse Core Ops, SparseCore 0:
  10.5 125.9 all-gather.1
where the time goes:
time: 219 us
  waiting for transfers between devices  113 us (52%)
  starting transfers between devices  36 us (16%)
  between operations  19.3 us (9%)
  matrix products  14.8 us (7%)
  other arithmetic  14.5 us (7%)
  blocking collectives  13.1 us (6%)
  local copies, waits for them, and re-layouts  8.21 us (4%)
    all_to_all x6, waiting for transfers between devices, copy_for_each(): return lax.all_to_all(copies, axis, split_axis=0, concat_axis=0, tiled=True)  69 us
    all_gather x1, waiting for transfers between devices, shards(): lax.all_gather(head_weight, 'fsdp', axis=0, tiled=True)  43.2 us
    all_to_all x6, starting transfers between devices, copy_for_each(): return lax.all_to_all(copies, axis, split_axis=0, concat_axis=0, tiled=True)  35.9 us
    dot_general x1, matrix products, shards(): jnp.dot(normed, lax.all_gather(head_weight, 'fsdp', axis=0, tiled=True),...  14.8 us
    all_to_all x1, blocking collectives, copy_for_each(): return lax.all_to_all(copies, axis, split_axis=0, concat_axis=0, tiled=True)  13.1 us
    reduce_sum x1, other arithmetic, exp_sums(): return (jnp.sum(shifted, axis=1), jnp.sum(shifted * shifted, axis=1))  5.43 us
    broadcast_in_dim x8, local copies, waits for them, and re-layouts, copy_for_each(): copies = jnp.broadcast_to(array, (lax.axis_size(axis), *array.shape))  5.14 us
  transfers between devices with their start and end apart: 7, of which 6 were waited for; matrix products, arithmetic and copies ran while one was open for 14% of the time, Pallas kernels for 0%

commit v1 on v0

--- a/solution.py
+++ b/solution.py
@@ -100,7 +100,9 @@
     tensor_pos = lax.axis_index("tensor")
     logits = jnp.dot(
         normed,
-        lax.all_gather(head_weight, "fsdp", axis=0, tiled=True),
+        jnp.concatenate(
+            lax.all_to_all(jnp.stack([head_weight] * lax.axis_size("fsdp")), "fsdp", 0, 0), axis=0
+        ),
         preferred_element_type=jnp.float32,
     )
     soft_stats = vocab_stats(logits, flat_ids, tensor_pos * vocab_cols)

time: 219 us -> 449 us (2.05)
  waiting for transfers between devices: 113 us -> 264 us
  blocking collectives: 13.1 us -> 67.8 us
  local copies, waits for them, and re-layouts: 8.21 us -> 34.6 us
  between operations: 19.3 us -> 5.9 us
  starting transfers between devices: 36 us -> 45.9 us
    all_to_all x0 -> x1, waiting for transfers between devices: none -> 246 us  [shards(): lax.all_to_all(jnp.stack([head_weight] * lax.axis_size('fsdp')), 'fsdp',...]
    all_to_all x1 -> x2, blocking collectives: 13.1 us -> 67.8 us  [copy_for_each(): return lax.all_to_all(copies, axis, split_axis=0, concat_axis=0, tiled=True)]
    all_to_all x6 -> x5, waiting for transfers between devices: 69 us -> 18.1 us  [copy_for_each(): return lax.all_to_all(copies, axis, split_axis=0, concat_axis=0, tiled=True)]
    all_gather x1 -> x0, waiting for transfers between devices: 43.2 us -> none  [shards(): lax.all_gather(head_weight, 'fsdp', axis=0, tiled=True)]
    all_to_all x0 -> x1, local copies, waits for them, and re-layouts: none -> 20.9 us  [shards(): lax.all_to_all(jnp.stack([head_weight] * lax.axis_size('fsdp')), 'fsdp',...]
    all_to_all x0 -> x1, starting transfers between devices: none -> 10.9 us  [shards(): lax.all_to_all(jnp.stack([head_weight] * lax.axis_size('fsdp')), 'fsdp',...]
    another operation x0 -> x1, local copies, waits for them, and re-layouts: none -> 6.85 us  [shards(): jnp.stack([head_weight] * lax.axis_size('fsdp'))]
    all_to_all x6 -> x5, starting transfers between devices: 35.9 us -> 35 us  [copy_for_each(): return lax.all_to_all(copies, axis, split_axis=0, concat_axis=0, tiled=True)]
  transfers between devices with their start and end apart: 7 -> 6, of which waited for: 6 -> 5; matrix products, arithmetic and copies ran while one was open for 14% -> 10% of each run, Pallas kernels for 0% -> 0%
where the time goes in v1:
time: 449 us; the launch traced here: 448 us
  waiting for transfers between devices  264 us (59%)
  blocking collectives  67.8 us (15%)
  starting transfers between devices  45.9 us (10%)
  local copies, waits for them, and re-layouts  34.6 us (8%)
  other arithmetic  14.5 us (3%)
  matrix products  14.4 us (3%)
  between operations  5.9 us (1%)
    all_to_all x1, waiting for transfers between devices, shards(): lax.all_to_all(jnp.stack([head_weight] * lax.axis_size('fsdp')), 'fsdp',...  246 us
    all_to_all x2, blocking collectives, copy_for_each(): return lax.all_to_all(copies, axis, split_axis=0, concat_axis=0, tiled=True)  67.8 us
    all_to_all x5, starting transfers between devices, copy_for_each(): return lax.all_to_all(copies, axis, split_axis=0, concat_axis=0, tiled=True)  35 us
    all_to_all x1, local copies, waits for them, and re-layouts, shards(): lax.all_to_all(jnp.stack([head_weight] * lax.axis_size('fsdp')), 'fsdp',...  20.9 us
    all_to_all x5, waiting for transfers between devices, copy_for_each(): return lax.all_to_all(copies, axis, split_axis=0, concat_axis=0, tiled=True)  18.1 us
    dot_general x1, matrix products, shards(): jnp.dot(normed, jnp.concatenate(lax.all_to_all(jnp.stack([head_weight] *...  14.4 us
    all_to_all x1, starting transfers between devices, shards(): lax.all_to_all(jnp.stack([head_weight] * lax.axis_size('fsdp')), 'fsdp',...  10.9 us
  transfers between devices with their start and end apart: 6, of which 5 were waited for; matrix products, arithmetic and copies ran while one was open for 10% of the time, Pallas kernels for 0%

profile of v1, /device:TPU:1, one launch (start us, length us, event | category | flops | bytes accessed | tf_op | source)
XLA Modules:
  0.0 447.5 jit_solution(17906040013475217199)
XLA Ops:
  0.6 0.7 broadcast_in_dim.42
  1.8 0.7 reduce.12
  2.5 0.6 reshape.225
  3.1 9.0 %all-to-all-start.1 = ((bf16[8,2,128]{2,1,0:T(2,128)(2,1)}), bf16[8,2,128]{2,1,0:T(2,128)(2,1)S(1)}, u32[]{:S(2)}, u32[]{:S(2)}) async-start(bf16[8,2,128]{2,1,0:T(2,128)(2,1)} %reshape.225), calls=%async_computation.1 | async-start | bytes 8192 | tf_op jit(solution)/shard_map/all_to_all | solution.py:14
  12.1 1.1 copy.20
  13.2 5.5 %all-to-all-done.1 = bf16[8,2,128]{2,1,0:T(2,128)(2,1)S(1)} async-done(((bf16[8,2,128]{2,1,0:T(2,128)(2,1)}), bf16[8,2,128]{2,1,0:T(2,128)(2,1)S(1)}, u32[]{:S(2)}, u32[]{:S(2)}) %all-to-all-start.1) | async-done | bytes 4128 | tf_op jit(solution)/shard_map/all_to_all | solution.py:14
  18.8 50.8 %all_to_all.44 = bf16[8,512,256]{1,2,0:T(8,128)(2,1)S(1)} all-to-all(bf16[8,512,256]{1,2,0:T(8,128)(2,1)S(1)} %broadcast_in_dim.41), channel_id=1, replica_groups=mesh['dp'=2,'fsdp'=16,'tensor'=8] {'tensor'}, dimensions={0} | all-to-all | bytes 4194304 | tf_op jit(solution)/shard_map/all_to_all | solution.py:14
  69.6 6.8 %stack.4 = bf16[16,128,4016]{1,2,0:T(8,128)(2,1)} broadcast(bf16[128,4016]{0,1:T(8,128)(2,1)} %param.11), dimensions={1,2} | broadcast | bytes 17477632 | tf_op jit(solution)/shard_map/stack | solution.py:104
  76.5 10.9 %all-to-all-start.2 = ((bf16[16,128,4016]{1,2,0:T(8,128)(2,1)}), bf16[16,128,4016]{1,2,0:T(8,128)(2,1)}, u32[]{:S(2)}, u32[]{:S(2)}) async-start(bf16[16,128,4016]{1,2,0:T(8,128)(2,1)} %stack.4), calls=%async_computation.2 | async-start | bytes 32899072 | tf_op jit(solution)/shard_map/all_to_all | solution.py:104
  88.6 1.9 fusion.3
  90.4 246.3 %all-to-all-done.2 = bf16[16,128,4016]{1,2,0:T(8,128)(2,1)} async-done(((bf16[16,128,4016]{1,2,0:T(8,128)(2,1)}), bf16[16,128,4016]{1,2,0:T(8,128)(2,1)}, u32[]{:S(2)}, u32[]{:S(2)}) %all-to-all-start.2) | async-done | bytes 16449568 | tf_op jit(solution)/shard_map/all_to_all | solution.py:104
  336.7 0.6 broadcast_in_dim.48
  337.3 13.8 %all-to-all-start.5 = ((f32[32,1,64]{2,1,0:T(1,128)}), f32[32,1,64]{2,1,0:T(1,128)S(1)}, u32[]{:S(2)}, u32[]{:S(2)}) async-start(f32[32,1,64]{2,1,0:T(1,128)} %broadcast_in_dim.48), calls=%async_computation.5 | async-start | bytes 32768 | tf_op jit(solution)/shard_map/all_to_all | solution.py:14
  351.1 20.9 %copy.21 = bf16[16,128,4016]{2,1,0:T(8,128)(2,1)} copy(bf16[16,128,4016]{1,2,0:T(8,128)(2,1)} %all-to-all-done.2) | data formatting | bytes 32899072 | tf_op jit(solution)/shard_map/all_to_all | solution.py:104
  372.0 14.4 %fusion.19 = (f32[512]{0:T(512)S(1)}, f32[512,4016]{0,1:T(8,128)}) fusion(bf16[512,2048]{0,1:T(8,128)(2,1)S(1)} %bitcast.28, bf16[2048,4016]{1,0:T(8,128)(2,1)} %bitcast.27), kind=kOutput, calls=%fused_computation.45 | convolution fusion | flops 8424218112 | bytes 26773504 | tf_op jit(solution)/shard_map/dot_general | solution.py:101
  386.4 0.6 broadcast_in_dim.43
  387.0 3.3 all-to-all-start.3
  390.4 6.5 %all-to-all-done.3 = f32[8,1,512]{2,1,0:T(1,128)S(1)} async-done(((f32[8,1,512]{2,1,0:T(1,128)}), f32[8,1,512]{2,1,0:T(1,128)S(1)}, u32[]{:S(2)}, u32[]{:S(2)}) %all-to-all-start.3) | async-done | bytes 16416 | tf_op jit(solution)/shard_map/all_to_all | solution.py:14
  396.9 0.6 broadcast_in_dim.50
  397.5 3.3 all-to-all-start.6
  400.9 5.5 %fusion = (f32[512]{0:T(512)S(1)}, f32[512]{0:T(512)S(1)}, f32[512]{0:T(512)S(1)}) fusion(f32[512,4016]{0,1:T(8,128)} %get-tuple-element.29, f32[512]{0:T(512)S(1)} %reduce_max.19, s32[512]{0:T(512)S(1)} %bitcast.36, s32[4016]{0:T(1024)S(1)} %iota_add_fusion), kind=kLoop, calls=%fused_computation.3 | loop fusion | flops 14391808 | bytes 8251072 | tf_op jit(solution)/shard_map/reduce_sum | solution.py:70
  406.4 1.0 all-to-all-done.6
  407.3 0.6 broadcast_in_dim.45
  408.0 5.6 %all-to-all-start.4 = ((f32[8,1,1536]{2,1,0:T(1,128)}), f32[8,1,1536]{2,1,0:T(1,128)S(1)}, u32[]{:S(2)}, u32[]{:S(2)}) async-start(f32[8,1,1536]{2,1,0:T(1,128)} %broadcast_in_dim.45), calls=%async_computation.4 | async-start | bytes 98304 | tf_op jit(solution)/shard_map/all_to_all | solution.py:14
  414.8 0.7 reduce.11
  415.5 5.1 %all-to-all-done.4 = f32[8,1,1536]{2,1,0:T(1,128)S(1)} async-done(((f32[8,1,1536]{2,1,0:T(1,128)}), f32[8,1,1536]{2,1,0:T(1,128)S(1)}, u32[]{:S(2)}, u32[]{:S(2)}) %all-to-all-start.4) | async-done | bytes 49184 | tf_op jit(solution)/shard_map/all_to_all | solution.py:14
  420.8 0.6 reduce_sum.97
  421.5 1.3 fusion.16
  422.8 2.6 pad_maximum_fusion.1
  425.4 17.0 %all_to_all.45 = f32[32,1,4]{2,1,0:T(1,128)S(1)} all-to-all(f32[32,1,4]{2,1,0:T(1,128)S(1)} %broadcast_in_dim.51), channel_id=1, replica_groups=mesh['dp'=2,'fsdp'=16,'tensor'=8] {'dp','fsdp'}, dimensions={0} | all-to-all | bytes 1024 | tf_op jit(solution)/shard_map/all_to_all | solution.py:14
  442.4 0.7 fusion.18
  446.9 0.6 pad_maximum_fusion.2
  (32 shorter events, 2.1 us)
Async XLA Ops:
  3.1 15.6 %all-to-all-start.1 = ((bf16[8,2,128]{2,1,0:T(2,128)(2,1)}), bf16[8,2,128]{2,1,0:T(2,128)(2,1)S(1)}, u32[]{:S(2)}, u32[]{:S(2)}) async-start(bf16[8,2,128]{2,1,0:T(2,128)(2,1)} %reshape.225), calls=%async_computation.1 | async-start | bytes 8192 | tf_op jit(solution)/shard_map/all_to_all | solution.py:14
  76.5 260.3 %copy-start.5 = (f32[1,64]{1,0:T(1,128)S(1)}, f32[1,64]{1,0:T(1,128)}, u32[]{:S(2)}) copy-start(f32[1,64]{1,0:T(1,128)} %param.16) | copy-start | bytes 772
  76.5 260.3 %all-to-all-start.2 = ((bf16[16,128,4016]{1,2,0:T(8,128)(2,1)}), bf16[16,128,4016]{1,2,0:T(8,128)(2,1)}, u32[]{:S(2)}, u32[]{:S(2)}) async-start(bf16[16,128,4016]{1,2,0:T(8,128)(2,1)} %stack.4), calls=%async_computation.2 | async-start | bytes 32899072 | tf_op jit(solution)/shard_map/all_to_all | solution.py:104
  337.3 49.1 %all-to-all-start.5 = ((f32[32,1,64]{2,1,0:T(1,128)}), f32[32,1,64]{2,1,0:T(1,128)S(1)}, u32[]{:S(2)}, u32[]{:S(2)}) async-start(f32[32,1,64]{2,1,0:T(1,128)} %broadcast_in_dim.48), calls=%async_computation.5 | async-start | bytes 32768 | tf_op jit(solution)/shard_map/all_to_all | solution.py:14
  351.1 20.9 %copy-start = (bf16[8,512,256]{1,2,0:T(8,128)(2,1)S(1)}, bf16[8,512,256]{1,2,0:T(8,128)(2,1)}, u32[]{:S(2)}) copy-start(bf16[8,512,256]{1,2,0:T(8,128)(2,1)} %fusion.3) | copy-start | bytes 6291460
  372.0 28.9 %copy-start.4 = (s32[1,512]{1,0:T(1,128)S(1)}, s32[1,512]{1,0:T(1,128)}, u32[]{:S(2)}) copy-start(s32[1,512]{1,0:T(1,128)} %param.12) | copy-start | bytes 6148
  386.4 35.1 %copy-start.2 = (f32[1,512]{1,0:T(1,128)S(1)}, f32[1,512]{1,0:T(1,128)}, u32[]{:S(2)}) copy-start(f32[1,512]{1,0:T(1,128)} %param.15) | copy-start | bytes 6148
  386.4 35.1 %copy-start.3 = (f32[1,512]{1,0:T(1,128)S(1)}, f32[1,512]{1,0:T(1,128)}, u32[]{:S(2)}) copy-start(f32[1,512]{1,0:T(1,128)} %param.14) | copy-start | bytes 6148
  387.0 9.9 %all-to-all-start.3 = ((f32[8,1,512]{2,1,0:T(1,128)}), f32[8,1,512]{2,1,0:T(1,128)S(1)}, u32[]{:S(2)}, u32[]{:S(2)}) async-start(f32[8,1,512]{2,1,0:T(1,128)} %broadcast_in_dim.43), calls=%async_computation.3 | async-start | bytes 32768 | tf_op jit(solution)/shard_map/all_to_all | solution.py:14
  397.5 9.8 %all-to-all-start.6 = ((f32[8,1,64]{2,1,0:T(1,128)}), f32[8,1,64]{2,1,0:T(1,128)S(1)}, u32[]{:S(2)}, u32[]{:S(2)}) async-start(f32[8,1,64]{2,1,0:T(1,128)} %broadcast_in_dim.50), calls=%async_computation.6 | async-start | bytes 8192 | tf_op jit(solution)/shard_map/all_to_all | solution.py:14
  408.0 12.7 %all-to-all-start.4 = ((f32[8,1,1536]{2,1,0:T(1,128)}), f32[8,1,1536]{2,1,0:T(1,128)S(1)}, u32[]{:S(2)}, u32[]{:S(2)}) async-start(f32[8,1,1536]{2,1,0:T(1,128)} %broadcast_in_dim.45), calls=%async_computation.4 | async-start | bytes 98304 | tf_op jit(solution)/shard_map/all_to_all | solution.py:14
  420.7 26.8 %copy-start.1 = (f32[512]{0:T(512)}, f32[512]{0:T(512)S(1)}, u32[]{:S(2)}) copy-start(f32[512]{0:T(512)S(1)} %get-tuple-element.20) | copy-start | bytes 6148
